TPU v7x, 32 devices: a whole 2x2x4 slice. The times are simulated.
32 devices in a mesh: cells: 16 (over z, y, x), faces: 2 (over core).
Axes of the slice: x: 2, y: 2, z: 4, core: 2. Of those that a mesh axis runs over, the one named last changes fastest.
Arguments:
- flow_state: float32 [4, 131072], P(None, 'cells'), may hold values from -6 to 6
- source_term: float32 [4, 131072], P(None, 'cells'), may hold values from -24 to 24
- volume_rate: float32 [131072], P('cells'), may hold values from 0.5 to 4
- face_normal: float32 [3, 393216], P(None, ('cells', 'faces')), may hold values from -3 to 3
- face_owner: int32 [393216], P(('cells', 'faces')), may hold values from 0 to 8191, as said below
- face_neighbour: int32 [393216], P(('cells', 'faces')), may hold values from 0 to 9727, as said below
- face_count: int32 [32], P(('cells', 'faces')), may hold values from 1536 to 12288, as said below
- send_list: int32 [96, 256], P('cells'), may hold values from 0 to 8191
- halo_count: int32 [96], P('cells'), may hold values from 64 to 256, as said below
Outputs:
- solution_field: float32 [4, 131072], P(None, 'cells')
- residual: float32 [4, 131072], P(None, 'cells')
Inputs may be any that keep to these rules, and one draw needn't show every extreme that they name: `face_owner`: A local cell of the slot's partition; with s = g mod 12288 and t = s // 192, it lies in 128 * t to 128 * t + 127. `face_neighbour`: with s and t as for face_owner: below 8192 a local cell (128 * t + d) mod 8192 with d in 0 to 255; otherwise 8192 plus a halo slot of the slot's partition in (t mod (6)) * 256 to that plus 256 - 1. Live slots of a block are its first face_count slots; in every draw some block has all 12288 slots live. `send_list`: entries at or past the list's count are unused. `halo_count`: every partition has one list with exactly 256 entries.
All inputs are finite; a program needn't handle non-finite values.
Results may differ from a plain program's by a relative error of at most 0.0003.
Values sent between devices are 32-bit elements; how exact they have to be, the bound alone decides.
No kernel may reach another device: no remote copies, remote signals or barrier semaphores. Data moves between devices by JAX's collectives and lax.ppermute only.
A program may use at most 64 MiB of HBM per device.

v0:
```python
import jax
import jax.numpy as jnp
import numpy as np
from jax import lax
from jax.sharding import PartitionSpec as P

ITERS = 2


def passed_along(block, axis, distance):
    devices = range(lax.axis_size(axis))
    route = [((i - distance) % len(devices), i) for i in devices]
    return lax.ppermute(block, axis, route)


def offsets(count):
    return [which + 1 for which in range(count)] + [-(which + 1) for which in range(count)]


def body(
    flow_state,
    source_term,
    volume_rate,
    face_normal,
    face_owner,
    face_neighbour,
    face_count,
    send_list,
    halo_count,
):
    highest = lax.Precision.HIGHEST
    cells_here = flow_state.shape[1]
    list_total, slot_width = send_list.shape
    shift_list = offsets(list_total // 2)
    slot_ids = lax.broadcasted_iota(jnp.int32, (list_total, slot_width), 1)
    keep_mask = (slot_ids < halo_count[:, None]).astype(jnp.float32)
    tiles = cells_here // 128
    slot_total = face_owner.shape[0]
    per_tile = slot_total // tiles
    halo_total = list_total * slot_width
    window = max(slot_width, halo_total // tiles)
    window_count = halo_total // window
    window_pick = np.arange(tiles) % window_count
    tile_ids = lax.broadcasted_iota(jnp.int32, (tiles, per_tile), 0)
    owner_tiled = face_owner.reshape(tiles, per_tile)
    neighbour_tiled = face_neighbour.reshape(tiles, per_tile)
    is_local_tiled = neighbour_tiled < cells_here
    owner_column = owner_tiled - tile_ids * 128
    local_column = jnp.where(is_local_tiled, (neighbour_tiled - tile_ids * 128) % cells_here, -1)
    halo_column = jnp.where(
        is_local_tiled, -1, neighbour_tiled - cells_here - tile_ids % window_count * window
    )
    owner_hot = (
        owner_column[:, :, None] == lax.broadcasted_iota(jnp.int32, (1, 1, 128), 2)
    ).astype(jnp.float32)
    local_hot = (
        local_column[:, :, None] == lax.broadcasted_iota(jnp.int32, (1, 1, 256), 2)
    ).astype(jnp.float32)
    halo_hot = (
        halo_column[:, :, None] == lax.broadcasted_iota(jnp.int32, (1, 1, window), 2)
    ).astype(jnp.float32)
    is_live = (
        lax.broadcasted_iota(jnp.int32, (tiles, per_tile), 0) * per_tile
        + lax.broadcasted_iota(jnp.int32, (tiles, per_tile), 1)
        < face_count[0]
    ).astype(jnp.float32)
    local_weight = is_local_tiled.astype(jnp.float32)
    normal_tiled = face_normal.reshape(3, tiles, per_tile)

    def ghosts(vector_in):
        outgoing = (
            jnp.stack(
                [jnp.take(vector_in, send_list[which], axis=1) for which in range(list_total)]
            )
            * keep_mask[:, None, :]
        )
        incoming = jnp.stack(
            [
                passed_along(outgoing[which], "cells", shift_list[which])
                for which in range(list_total)
            ]
        )
        return jnp.transpose(incoming, (1, 0, 2)).reshape(vector_in.shape[0], halo_total)

    def to_faces(vector_in):
        rows = vector_in.shape[0]
        blocks = vector_in.reshape(rows, tiles, 128)
        paired = jnp.concatenate([blocks, jnp.roll(blocks, -1, axis=1)], axis=2)
        halo_cells = ghosts(vector_in)
        halo_windows = halo_cells.reshape(rows, window_count, window)[:, window_pick]
        left_side = jnp.einsum("tfc,btc->btf", owner_hot, blocks, precision=highest)
        right_side = jnp.einsum("tfc,btc->btf", local_hot, paired, precision=highest)
        right_side = right_side + jnp.einsum(
            "tfc,btc->btf", halo_hot, halo_windows, precision=highest
        )
        return (left_side, right_side)

    def to_cells(owner_values, neighbour_values):
        rows = owner_values.shape[0]
        owned = jnp.einsum("tfc,btf->btc", owner_hot, owner_values, precision=highest)
        beside = jnp.einsum("tfc,btf->btc", local_hot, neighbour_values, precision=highest)
        summed = owned + beside[:, :, :128] + jnp.roll(beside[:, :, 128:], 1, axis=1)
        return summed.reshape(rows, cells_here)

    left_state, right_state = to_faces(flow_state)
    normal_speed = 0.5 * jnp.sum(normal_tiled * (left_state[:3] + right_state[:3]), axis=0)
    normal_size = jnp.sqrt(jnp.sum(normal_tiled * normal_tiled, axis=0))
    wave_speed = jnp.abs(normal_speed) + 2.0 * normal_size
    owner_terms = (
        0.5
        * jnp.concatenate([normal_speed[None], normal_tiled, wave_speed[None]], axis=0)
        * is_live
    )
    neighbour_terms = jnp.concatenate(
        [-0.5 * normal_speed[None], -0.5 * normal_tiled, 0.5 * wave_speed[None]], axis=0
    ) * (is_live * local_weight)
    block_terms = lax.psum(to_cells(owner_terms, neighbour_terms), "faces")
    velocity_diag = volume_rate + block_terms[0] + block_terms[4]
    pressure_diag = volume_rate + block_terms[4]
    coupling = block_terms[1:4]
    schur = pressure_diag - jnp.sum(coupling * coupling, axis=0) / velocity_diag

    def precondition(vector_in):
        pressure = (
            vector_in[3] - jnp.sum(coupling * vector_in[:3], axis=0) / velocity_diag
        ) / schur
        velocity = (vector_in[:3] - coupling * pressure) / velocity_diag
        return jnp.concatenate([velocity, pressure[None]], axis=0)

    def apply_matrix(vector_in):
        left_side, right_side = to_faces(vector_in)
        face_sum = left_side + right_side
        central = jnp.concatenate(
            [
                normal_speed * face_sum[:3] + normal_tiled * face_sum[3],
                jnp.sum(normal_tiled * face_sum[:3], axis=0)[None],
            ],
            axis=0,
        )
        face_flux = (0.5 * central - 0.5 * wave_speed * (right_side - left_side)) * is_live
        partial_value = to_cells(face_flux, -face_flux * local_weight)
        return volume_rate * vector_in + lax.psum(partial_value, "faces")

    solution_field = jnp.zeros_like(source_term)
    residual = source_term
    direction = source_term
    rho_now = lax.psum(jnp.sum(source_term * residual), "cells")
    for iteration in range(ITERS):
        pre_dir = precondition(direction)
        image = apply_matrix(pre_dir)
        step_alpha = rho_now / lax.psum(jnp.sum(source_term * image), "cells")
        middle = residual - step_alpha * image
        pre_mid = precondition(middle)
        second = apply_matrix(pre_mid)
        second_mid, second_sq, shadow_mid, shadow_second = lax.psum(
            (
                jnp.sum(second * middle),
                jnp.sum(second * second),
                jnp.sum(source_term * middle),
                jnp.sum(source_term * second),
            ),
            "cells",
        )
        step_omega = second_mid / second_sq
        solution_field = solution_field + step_alpha * pre_dir + step_omega * pre_mid
        residual = middle - step_omega * second
        rho_next = shadow_mid - step_omega * shadow_second
        if iteration + 1 < ITERS:
            ratio_beta = rho_next / rho_now * (step_alpha / step_omega)
            direction = residual + ratio_beta * (direction - step_omega * image)
            rho_now = rho_next
    return (solution_field, residual)


def solution(mesh):
    in_specs = (
        P(None, "cells"),
        P(None, "cells"),
        P("cells"),
        P(None, ("cells", "faces")),
        P(("cells", "faces")),
        P(("cells", "faces")),
        P(("cells", "faces")),
        P("cells", None),
        P("cells"),
    )
    out_specs = (P(None, "cells"), P(None, "cells"))
    return jax.shard_map(body, mesh=mesh, in_specs=in_specs, out_specs=out_specs, check_vma=False)
```

profile of v0, /device:TPU:0, one launch (start us, length us, event | category | flops | bytes accessed | tf_op | source)
XLA Modules:
  0.0 638.8 jit_solution(4085861947890233693)
XLA Ops:
  42.0 6.4 fusion.61
  54.7 6.8 %fusion.4 = f32[64,4,192]{2,1,0:T(4,128)S(1)} fusion(s32[64,192]{1,0:T(8,128)S(1)} %get-tuple-element.48, f32[64,4,256]{2,1,0:T(4,128)S(1)} %gather_fusion), kind=kOutput, calls=%fused_computation.40 | convolution fusion | flops 154140672 | bytes 507904 | tf_op jit(solution)/shard_map/tfc,btc->btf/dot_general | solution.py:93
  61.5 6.9 %fusion.56 = f32[4,64,192]{2,0,1:T(4,128)S(1)} fusion(f32[64,4,192]{2,1,0:T(4,128)S(1)} %fusion.4, s32[64,192]{1,0:T(8,128)S(1)} %get-tuple-element.47, f32[4,1,128]{2,0,1:T(4,128)S(1)} %slice.454, f32[4,63,128]{2,0,1:T(4,128)S(1)} %slice.453, f32[4,64,128]{2,0,1:T(4,128)S(1)} %bitcast.444), kind=kOutput, calls=%fused_computation.94 | convolution fusion | flops 154320896 | bytes 704512 | tf_op jit(solution)/shard_map/tfc,btc->btf/dot_general | solution.py:92
  68.8 6.9 %fusion.50 = f32[5,64,256]{2,0,1:T(8,128)S(1)} fusion(s32[64,192]{1,0:T(8,128)S(1)} %get-tuple-element.47, f32[5,64,192]{2,1,0:T(8,128)S(1)} %maximum_multiply_fusion.1), kind=kOutput, calls=%fused_computation.88 | convolution fusion | flops 191889408 | bytes 622592 | tf_op jit(solution)/shard_map/tfc,btf->btc/dot_general | solution.py:101
  81.3 18.1 %all-reduce.9.cloned.1.call-done = f32[5,8192]{1,0:T(8,128)} async-done(((f32[5,8192]{1,0:T(8,128)}), f32[5,8192]{1,0:T(8,128)}) %all-reduce.9.cloned.1.call-update) | async-done | bytes 163856 | tf_op jit(solution)/shard_map/psum | solution.py:117
  123.0 6.4 fusion.37
  145.3 6.8 %fusion.3 = f32[64,4,192]{2,1,0:T(4,128)S(1)} fusion(s32[64,192]{1,0:T(8,128)S(1)} %get-tuple-element.48, f32[64,4,256]{2,1,0:T(4,128)S(1)} %gather_fusion.1), kind=kOutput, calls=%fused_computation.39 | convolution fusion | flops 154140672 | bytes 507904 | tf_op jit(solution)/shard_map/tfc,btc->btf/dot_general | solution.py:93
  152.1 6.9 %fusion.57 = f32[64,4,192]{2,1,0:T(4,128)S(1)} fusion(f32[64,4,192]{2,1,0:T(4,128)S(1)} %fusion.3, s32[64,192]{1,0:T(8,128)S(1)} %get-tuple-element.47, f32[4,1,128]{2,0,1:T(4,128)S(1)} %fusion.167, f32[4,63,128]{2,0,1:T(4,128)S(1)} %fusion.154, f32[1,64,128]{2,0,1:T(1,128)S(1)} %bitcast.425, f32[3,64,128]{2,0,1:T(4,128)S(1)} %bitcast.399), kind=kOutput, calls=%fused_computation.95 | convolution fusion | flops 154386432 | bytes 704512 | tf_op jit(solution)/shard_map/tfc,btc->btf/dot_general | solution.py:92
  170.6 17.9 %all-reduce.11.cloned.1.call-done = f32[4,8192]{1,0:T(4,128)} async-done(((f32[4,8192]{1,0:T(4,128)}), f32[4,8192]{1,0:T(4,128)}) %all-reduce.11.cloned.1.call-update) | async-done | bytes 131088 | tf_op jit(solution)/shard_map/psum | solution.py:142
  190.2 42.6 %all-reduce.2 = (f32[]{:T(128)}, f32[]{:T(128)}) all-reduce(f32[]{:T(128)} %get-tuple-element.16, f32[]{:T(128)} %get-tuple-element.15), channel_id=1, replica_groups=mesh['cells'=16,'faces'=2] {'cells'}, use_global_device_ids=true, to_apply=%region_1.2 | all-reduce | flops 2 | bytes 16 | tf_op jit(solution)/shard_map/psum | solution.py:147
  254.6 6.4 fusion.35
  275.2 6.8 %fusion.2 = f32[64,4,192]{2,1,0:T(4,128)S(1)} fusion(s32[64,192]{1,0:T(8,128)S(1)} %get-tuple-element.48, f32[64,4,256]{2,1,0:T(4,128)S(1)} %gather_fusion.2), kind=kOutput, calls=%fused_computation.38 | convolution fusion | flops 154140672 | bytes 507904 | tf_op jit(solution)/shard_map/tfc,btc->btf/dot_general | solution.py:93
  282.0 6.9 %fusion.58 = f32[64,4,192]{2,1,0:T(4,128)S(1)} fusion(f32[64,4,192]{2,1,0:T(4,128)S(1)} %fusion.2, s32[64,192]{1,0:T(8,128)S(1)} %get-tuple-element.47, f32[4,1,128]{2,0,1:T(4,128)S(1)} %fusion.166, f32[4,63,128]{2,0,1:T(4,128)S(1)} %fusion.153, f32[1,64,128]{2,0,1:T(1,128)S(1)} %bitcast.432, f32[3,64,128]{2,0,1:T(4,128)S(1)} %bitcast.403), kind=kOutput, calls=%fused_computation.96 | convolution fusion | flops 154386432 | bytes 704512 | tf_op jit(solution)/shard_map/tfc,btc->btf/dot_general | solution.py:92
  300.4 18.5 %all-reduce.13.cloned.1.call-done = f32[4,8192]{1,0:T(4,128)} async-done(((f32[4,8192]{1,0:T(4,128)}), f32[4,8192]{1,0:T(4,128)}) %all-reduce.13.cloned.1.call-update) | async-done | bytes 131088 | tf_op jit(solution)/shard_map/psum | solution.py:142
  320.7 42.9 %all-reduce.1 = (f32[]{:T(128)}, f32[]{:T(128)}, f32[]{:T(128)}, f32[]{:T(128)}) all-reduce(f32[]{:T(128)} %get-tuple-element.14, f32[]{:T(128)} %get-tuple-element.13, f32[]{:T(128)} %get-tuple-element.12, f32[]{:T(128)} %get-tuple-element.11), channel_id=1, replica_groups=mesh['cells'=16,'faces'=2] {'cells'}, use_global_device_ids=true, to_apply=%region_19.21 | all-reduce | flops 4 | bytes 32 | tf_op jit(solution)/shard_map/psum | solution.py:155
  389.9 6.4 fusion.33
  410.5 6.8 %fusion.1 = f32[64,4,192]{2,1,0:T(4,128)S(1)} fusion(s32[64,192]{1,0:T(8,128)S(1)} %get-tuple-element.48, f32[64,4,256]{2,1,0:T(4,128)S(1)} %gather_fusion.3), kind=kOutput, calls=%fused_computation.37 | convolution fusion | flops 154140672 | bytes 507904 | tf_op jit(solution)/shard_map/tfc,btc->btf/dot_general | solution.py:93
  417.3 6.9 %fusion.59 = f32[64,4,192]{2,1,0:T(4,128)S(1)} fusion(f32[64,4,192]{2,1,0:T(4,128)S(1)} %fusion.1, s32[64,192]{1,0:T(8,128)S(1)} %get-tuple-element.47, f32[4,1,128]{2,0,1:T(4,128)S(1)} %fusion.165, f32[4,63,128]{2,0,1:T(4,128)S(1)} %fusion.152, f32[1,64,128]{2,0,1:T(1,128)S(1)} %bitcast.417, f32[3,64,128]{2,0,1:T(4,128)S(1)} %bitcast.395), kind=kOutput, calls=%fused_computation.97 | convolution fusion | flops 154386432 | bytes 704512 | tf_op jit(solution)/shard_map/tfc,btc->btf/dot_general | solution.py:92
  435.8 18.5 %all-reduce.15.cloned.1.call-done = f32[4,8192]{1,0:T(4,128)} async-done(((f32[4,8192]{1,0:T(4,128)}), f32[4,8192]{1,0:T(4,128)}) %all-reduce.15.cloned.1.call-update) | async-done | bytes 131088 | tf_op jit(solution)/shard_map/psum | solution.py:142
  455.9 42.6 %psum.108 = f32[]{:T(128)} all-reduce(f32[]{:T(128)} %multiply_reduce_fusion.4), channel_id=1, replica_groups=mesh['cells'=16,'faces'=2] {'cells'}, use_global_device_ids=true, to_apply=%region_26.28 | all-reduce | flops 1 | bytes 8 | tf_op jit(solution)/shard_map/psum | solution.py:151
  541.3 6.8 %fusion = f32[64,4,192]{2,1,0:T(4,128)S(1)} fusion(s32[64,192]{1,0:T(8,128)S(1)} %get-tuple-element.48, f32[64,4,256]{2,1,0:T(4,128)S(1)} %gather_fusion.4), kind=kOutput, calls=%fused_computation.36 | convolution fusion | flops 154140672 | bytes 507904 | tf_op jit(solution)/shard_map/tfc,btc->btf/dot_general | solution.py:93
  548.1 6.9 %fusion.60 = f32[64,4,192]{2,1,0:T(4,128)S(1)} fusion(f32[64,4,192]{2,1,0:T(4,128)S(1)} %fusion, s32[64,192]{1,0:T(8,128)S(1)} %get-tuple-element.47, f32[4,1,128]{2,0,1:T(4,128)S(1)} %fusion.164, f32[4,63,128]{2,0,1:T(4,128)S(1)} %fusion.151, f32[1,64,128]{2,0,1:T(1,128)S(1)} %bitcast.439, f32[3,64,128]{2,0,1:T(4,128)S(1)} %bitcast.407), kind=kOutput, calls=%fused_computation.98 | convolution fusion | flops 154386432 | bytes 704512 | tf_op jit(solution)/shard_map/tfc,btc->btf/dot_general | solution.py:92
  566.5 18.6 %all-reduce.17.cloned.1.call-done = f32[4,8192]{1,0:T(4,128)} async-done(((f32[4,8192]{1,0:T(4,128)}), f32[4,8192]{1,0:T(4,128)}) %all-reduce.17.cloned.1.call-update) | async-done | bytes 131088 | tf_op jit(solution)/shard_map/psum | solution.py:142
  586.7 42.6 %all-reduce = (f32[]{:T(128)}, f32[]{:T(128)}) all-reduce(f32[]{:T(128)} %get-tuple-element.10, f32[]{:T(128)} %get-tuple-element.9), channel_id=1, replica_groups=mesh['cells'=16,'faces'=2] {'cells'}, use_global_device_ids=true, to_apply=%region_31.33 | all-reduce | flops 2 | bytes 16 | tf_op jit(solution)/shard_map/psum | solution.py:155
  (381 shorter events, 250.8 us)
Async XLA Ops:
  7.2 92.2 %all-reduce.9.cloned.1.call-start = ((), (), s32[]{:S(2)}) async-start(), calls=%async_computation | async-start | bytes 524288 | tf_op jit(solution)/shard_map/psum | solution.py:117
  30.6 18.8 %collective-permute-start = (f32[4,256]{1,0:T(4,128)S(1)}, f32[4,256]{1,0:T(4,128)S(1)}, u32[]{:S(2)}, u32[]{:S(2)}) collective-permute-start(f32[4,256]{1,0:T(4,128)S(1)} %get-tuple-element.78), channel_id=1, source_target_pairs={{30,0},{0,2},{2,4},{4,6},{6,8},{8,10},{10,12},{12,14},{14,16},{16,... | collective-permute-start | bytes 12296 | tf_op jit(solution)/shard_map/ppermute | solution.py:13
  33.7 17.1 %collective-permute-start.1 = (f32[4,256]{1,0:T(4,128)S(1)}, f32[4,256]{1,0:T(4,128)S(1)}, u32[]{:S(2)}, u32[]{:S(2)}) collective-permute-start(f32[4,256]{1,0:T(4,128)S(1)} %get-tuple-element.77), channel_id=1, source_target_pairs={{28,0},{30,2},{0,4},{2,6},{4,8},{6,10},{8,12},{10,14},{12,16},{14,... | collective-permute-start | bytes 12296 | tf_op jit(solution)/shard_map/ppermute | solution.py:13
  35.2 15.6 %collective-permute-start.2 = (f32[4,256]{1,0:T(4,128)S(1)}, f32[4,256]{1,0:T(4,128)S(1)}, u32[]{:S(2)}, u32[]{:S(2)}) collective-permute-start(f32[4,256]{1,0:T(4,128)S(1)} %get-tuple-element.76), channel_id=1, source_target_pairs={{26,0},{28,2},{30,4},{0,6},{2,8},{4,10},{6,12},{8,14},{10,16},{12,... | collective-permute-start | bytes 12296 | tf_op jit(solution)/shard_map/ppermute | solution.py:13
  37.6 13.2 %collective-permute-start.3 = (f32[4,256]{1,0:T(4,128)S(1)}, f32[4,256]{1,0:T(4,128)S(1)}, u32[]{:S(2)}, u32[]{:S(2)}) collective-permute-start(f32[4,256]{1,0:T(4,128)S(1)} %get-tuple-element.75), channel_id=1, source_target_pairs={{2,0},{4,2},{6,4},{8,6},{10,8},{12,10},{14,12},{16,14},{18,16},{20... | collective-permute-start | bytes 12296 | tf_op jit(solution)/shard_map/ppermute | solution.py:13
  40.9 10.0 %collective-permute-start.4 = (f32[4,256]{1,0:T(4,128)S(1)}, f32[4,256]{1,0:T(4,128)S(1)}, u32[]{:S(2)}, u32[]{:S(2)}) collective-permute-start(f32[4,256]{1,0:T(4,128)S(1)} %get-tuple-element.74), channel_id=1, source_target_pairs={{4,0},{6,2},{8,4},{10,6},{12,8},{14,10},{16,12},{18,14},{20,16},{2... | collective-permute-start | bytes 12296 | tf_op jit(solution)/shard_map/ppermute | solution.py:13
  81.2 107.3 %all-reduce.11.cloned.1.call-start = ((), (), s32[]{:S(2)}) async-start(), calls=%async_computation.1 | async-start | bytes 262144 | tf_op jit(solution)/shard_map/psum | solution.py:142
  130.6 9.5 %collective-permute-start.6 = (f32[4,256]{1,0:T(4,128)S(1)}, f32[4,256]{1,0:T(4,128)S(1)}, u32[]{:S(2)}, u32[]{:S(2)}) collective-permute-start(f32[4,256]{1,0:T(4,128)S(1)} %get-tuple-element.72), channel_id=1, source_target_pairs={{30,0},{0,2},{2,4},{4,6},{6,8},{8,10},{10,12},{12,14},{14,16},{16,... | collective-permute-start | bytes 12296 | tf_op jit(solution)/shard_map/ppermute | solution.py:13
  132.4 8.8 %collective-permute-start.7 = (f32[4,256]{1,0:T(4,128)S(1)}, f32[4,256]{1,0:T(4,128)S(1)}, u32[]{:S(2)}, u32[]{:S(2)}) collective-permute-start(f32[4,256]{1,0:T(4,128)S(1)} %get-tuple-element.71), channel_id=1, source_target_pairs={{28,0},{30,2},{0,4},{2,6},{4,8},{6,10},{8,12},{10,14},{12,16},{14,... | collective-permute-start | bytes 12296 | tf_op jit(solution)/shard_map/ppermute | solution.py:13
  170.5 148.4 %all-reduce.13.cloned.1.call-start = ((), (), s32[]{:S(2)}) async-start(), calls=%async_computation.2 | async-start | bytes 262144 | tf_op jit(solution)/shard_map/psum | solution.py:142
  262.2 7.7 %collective-permute-start.12 = (f32[4,256]{1,0:T(4,128)S(1)}, f32[4,256]{1,0:T(4,128)S(1)}, u32[]{:S(2)}, u32[]{:S(2)}) collective-permute-start(f32[4,256]{1,0:T(4,128)S(1)} %get-tuple-element.66), channel_id=1, source_target_pairs={{30,0},{0,2},{2,4},{4,6},{6,8},{8,10},{10,12},{12,14},{14,16},{16,... | collective-permute-start | bytes 12296 | tf_op jit(solution)/shard_map/ppermute | solution.py:13
  262.3 10.6 %collective-permute-start.13 = (f32[4,256]{1,0:T(4,128)S(1)}, f32[4,256]{1,0:T(4,128)S(1)}, u32[]{:S(2)}, u32[]{:S(2)}) collective-permute-start(f32[4,256]{1,0:T(4,128)S(1)} %get-tuple-element.65), channel_id=1, source_target_pairs={{28,0},{30,2},{0,4},{2,6},{4,8},{6,10},{8,12},{10,14},{12,16},{14,... | collective-permute-start | bytes 12296 | tf_op jit(solution)/shard_map/ppermute | solution.py:13
  262.4 10.5 %collective-permute-start.14 = (f32[4,256]{1,0:T(4,128)S(1)}, f32[4,256]{1,0:T(4,128)S(1)}, u32[]{:S(2)}, u32[]{:S(2)}) collective-permute-start(f32[4,256]{1,0:T(4,128)S(1)} %get-tuple-element.64), channel_id=1, source_target_pairs={{26,0},{28,2},{30,4},{0,6},{2,8},{4,10},{6,12},{8,14},{10,16},{12,... | collective-permute-start | bytes 12296 | tf_op jit(solution)/shard_map/ppermute | solution.py:13
  262.4 10.5 %collective-permute-start.15 = (f32[4,256]{1,0:T(4,128)S(1)}, f32[4,256]{1,0:T(4,128)S(1)}, u32[]{:S(2)}, u32[]{:S(2)}) collective-permute-start(f32[4,256]{1,0:T(4,128)S(1)} %get-tuple-element.63), channel_id=1, source_target_pairs={{2,0},{4,2},{6,4},{8,6},{10,8},{12,10},{14,12},{16,14},{18,16},{20... | collective-permute-start | bytes 12296 | tf_op jit(solution)/shard_map/ppermute | solution.py:13
  300.4 153.9 %all-reduce.15.cloned.1.call-start = ((), (), s32[]{:S(2)}) async-start(), calls=%async_computation.3 | async-start | bytes 262144 | tf_op jit(solution)/shard_map/psum | solution.py:142
  397.5 7.7 %collective-permute-start.18 = (f32[4,256]{1,0:T(4,128)S(1)}, f32[4,256]{1,0:T(4,128)S(1)}, u32[]{:S(2)}, u32[]{:S(2)}) collective-permute-start(f32[4,256]{1,0:T(4,128)S(1)} %get-tuple-element.60), channel_id=1, source_target_pairs={{30,0},{0,2},{2,4},{4,6},{6,8},{8,10},{10,12},{12,14},{14,16},{16,... | collective-permute-start | bytes 12296 | tf_op jit(solution)/shard_map/ppermute | solution.py:13
  397.6 10.6 %collective-permute-start.19 = (f32[4,256]{1,0:T(4,128)S(1)}, f32[4,256]{1,0:T(4,128)S(1)}, u32[]{:S(2)}, u32[]{:S(2)}) collective-permute-start(f32[4,256]{1,0:T(4,128)S(1)} %get-tuple-element.59), channel_id=1, source_target_pairs={{28,0},{30,2},{0,4},{2,6},{4,8},{6,10},{8,12},{10,14},{12,16},{14,... | collective-permute-start | bytes 12296 | tf_op jit(solution)/shard_map/ppermute | solution.py:13
  397.7 10.5 %collective-permute-start.20 = (f32[4,256]{1,0:T(4,128)S(1)}, f32[4,256]{1,0:T(4,128)S(1)}, u32[]{:S(2)}, u32[]{:S(2)}) collective-permute-start(f32[4,256]{1,0:T(4,128)S(1)} %get-tuple-element.58), channel_id=1, source_target_pairs={{26,0},{28,2},{30,4},{0,6},{2,8},{4,10},{6,12},{8,14},{10,16},{12,... | collective-permute-start | bytes 12296 | tf_op jit(solution)/shard_map/ppermute | solution.py:13
  397.7 10.5 %collective-permute-start.21 = (f32[4,256]{1,0:T(4,128)S(1)}, f32[4,256]{1,0:T(4,128)S(1)}, u32[]{:S(2)}, u32[]{:S(2)}) collective-permute-start(f32[4,256]{1,0:T(4,128)S(1)} %get-tuple-element.57), channel_id=1, source_target_pairs={{2,0},{4,2},{6,4},{8,6},{10,8},{12,10},{14,12},{16,14},{18,16},{20... | collective-permute-start | bytes 12296 | tf_op jit(solution)/shard_map/ppermute | solution.py:13
  435.7 149.3 %all-reduce.17.cloned.1.call-start = ((), (), s32[]{:S(2)}) async-start(), calls=%async_computation.4 | async-start | bytes 262144 | tf_op jit(solution)/shard_map/psum | solution.py:142
  528.3 7.7 %collective-permute-start.24 = (f32[4,256]{1,0:T(4,128)S(1)}, f32[4,256]{1,0:T(4,128)S(1)}, u32[]{:S(2)}, u32[]{:S(2)}) collective-permute-start(f32[4,256]{1,0:T(4,128)S(1)} %get-tuple-element.54), channel_id=1, source_target_pairs={{30,0},{0,2},{2,4},{4,6},{6,8},{8,10},{10,12},{12,14},{14,16},{16,... | collective-permute-start | bytes 12296 | tf_op jit(solution)/shard_map/ppermute | solution.py:13
  528.4 10.6 %collective-permute-start.25 = (f32[4,256]{1,0:T(4,128)S(1)}, f32[4,256]{1,0:T(4,128)S(1)}, u32[]{:S(2)}, u32[]{:S(2)}) collective-permute-start(f32[4,256]{1,0:T(4,128)S(1)} %get-tuple-element.53), channel_id=1, source_target_pairs={{28,0},{30,2},{0,4},{2,6},{4,8},{6,10},{8,12},{10,14},{12,16},{14,... | collective-permute-start | bytes 12296 | tf_op jit(solution)/shard_map/ppermute | solution.py:13
  528.5 10.5 %collective-permute-start.26 = (f32[4,256]{1,0:T(4,128)S(1)}, f32[4,256]{1,0:T(4,128)S(1)}, u32[]{:S(2)}, u32[]{:S(2)}) collective-permute-start(f32[4,256]{1,0:T(4,128)S(1)} %get-tuple-element.52), channel_id=1, source_target_pairs={{26,0},{28,2},{30,4},{0,6},{2,8},{4,10},{6,12},{8,14},{10,16},{12,... | collective-permute-start | bytes 12296 | tf_op jit(solution)/shard_map/ppermute | solution.py:13
  528.5 10.5 %collective-permute-start.27 = (f32[4,256]{1,0:T(4,128)S(1)}, f32[4,256]{1,0:T(4,128)S(1)}, u32[]{:S(2)}, u32[]{:S(2)}) collective-permute-start(f32[4,256]{1,0:T(4,128)S(1)} %get-tuple-element.51), channel_id=1, source_target_pairs={{2,0},{4,2},{6,4},{8,6},{10,8},{12,10},{14,12},{16,14},{18,16},{20... | collective-permute-start | bytes 12296 | tf_op jit(solution)/shard_map/ppermute | solution.py:13
  (20 other events, 392.6 us)
Sparse Core Ops, SparseCore 0:
  81.3 18.0 all-reduce.8
  170.7 17.8 all-reduce.10
  300.5 18.3 all-reduce.12
  435.8 18.3 all-reduce.14
  566.6 18.3 all-reduce.16
where the time goes:
time: 640 us; the launch traced here: 639 us
  blocking collectives  171 us (27%)
  matrix products  155 us (24%)
  local copies, waits for them, and re-layouts  111 us (17%)
  waiting for transfers between devices  103 us (16%)
  starting transfers between devices  54.7 us (9%)
  between operations  24.9 us (4%)
  other arithmetic  19.9 us (3%)
    gather x30, local copies, waits for them, and re-layouts, ghosts(): jnp.take(vector_in, send_list[which], axis=1)  87.3 us
    psum x2, blocking collectives, body(): lax.psum((jnp.sum(second * middle), jnp.sum(second * second), jnp.sum(sou...  85.5 us
    psum x4, waiting for transfers between devices, apply_matrix(): return volume_rate * vector_in + lax.psum(partial_value, 'faces')  73.5 us
    ppermute x30, starting transfers between devices, passed_along(): return lax.ppermute(block, axis, route)  54.5 us
    psum x1, blocking collectives, body(): rho_now = lax.psum(jnp.sum(source_term * residual), 'cells')  42.6 us
    psum x1, blocking collectives, body(): step_alpha = rho_now / lax.psum(jnp.sum(source_term * image), 'cells')  42.6 us
    dot_general x5, matrix products, to_faces(): jnp.einsum('tfc,btc->btf', local_hot, paired, precision=highest)  34.4 us
    dot_general x5, matrix products, to_faces(): jnp.einsum('tfc,btc->btf', halo_hot, halo_windows, precision=highest)  34 us
  transfers between devices with their start and end apart: 35, of which 11 were waited for; matrix products, arithmetic and copies ran while one was open for 1% of the time, Pallas kernels for 0%

commit v1 on v0

--- a/solution.py
+++ b/solution.py
@@ -139,7 +139,7 @@
         )
         face_flux = (0.5 * central - 0.5 * wave_speed * (right_side - left_side)) * is_live
         partial_value = to_cells(face_flux, -face_flux * local_weight)
-        return volume_rate * vector_in + lax.psum(partial_value, "faces")
+        return volume_rate * vector_in + jnp.sum(lax.all_gather(partial_value, "faces"), axis=0)
 
     solution_field = jnp.zeros_like(source_term)
     residual = source_term

time: 640 us -> 560 us (0.88)
  waiting for transfers between devices: 103 us -> 29.2 us
    psum x4 -> x0, waiting for transfers between devices: 73.5 us -> none  [apply_matrix(): return volume_rate * vector_in + lax.psum(partial_value, 'faces')]
    all_gather x0 -> x4, blocking collectives: none -> 7.97 us  [apply_matrix(): lax.all_gather(partial_value, 'faces')]
  transfers between devices with their start and end apart: 35 -> 31, of which waited for: 11 -> 7; matrix products, arithmetic and copies ran while one was open for 1% -> 1% of each run, Pallas kernels for 0% -> 0%
where the time goes in v1:
time: 560 us; the launch traced here: 558 us
  blocking collectives  170 us (30%)
  matrix products  152 us (27%)
  local copies, waits for them, and re-layouts  111 us (20%)
  starting transfers between devices  54.5 us (10%)
  waiting for transfers between devices  29.2 us (5%)
  between operations  25.2 us (4%)
  other arithmetic  15.8 us (3%)
    gather x30, local copies, waits for them, and re-layouts, ghosts(): jnp.take(vector_in, send_list[which], axis=1)  87.3 us
    psum x2, blocking collectives, body(): lax.psum((jnp.sum(second * middle), jnp.sum(second * second), jnp.sum(sou...  81.3 us
    ppermute x30, starting transfers between devices, passed_along(): return lax.ppermute(block, axis, route)  54.5 us
    psum x1, blocking collectives, body(): step_alpha = rho_now / lax.psum(jnp.sum(source_term * image), 'cells')  40.5 us
    psum x1, blocking collectives, body(): rho_now = lax.psum(jnp.sum(source_term * residual), 'cells')  40.4 us
    dot_general x5, matrix products, to_faces(): jnp.einsum('tfc,btc->btf', local_hot, paired, precision=highest)  34.4 us
    dot_general x5, matrix products, to_faces(): jnp.einsum('tfc,btc->btf', halo_hot, halo_windows, precision=highest)  34 us
    dot_general x5, matrix products, to_faces(): left_side = jnp.einsum('tfc,btc->btf', owner_hot, blocks, precision=highest)  31.8 us
  transfers between devices with their start and end apart: 31, of which 7 were waited for; matrix products, arithmetic and copies ran while one was open for 1% of the time, Pallas kernels for 0%

profile of v1, /device:TPU:0, one launch (start us, length us, event | category | flops | bytes accessed | tf_op | source)
XLA Modules:
  0.0 558.1 jit_solution(13733861067441319154)
XLA Ops:
  42.0 6.4 %fusion.61 = f32[4,64,192]{2,0,1:T(4,128)S(1)} fusion(s32[64,192]{1,0:T(8,128)S(1)} %get-tuple-element.87, f32[4,8192]{1,0:T(4,128)S(1)} %copy-done.4), kind=kOutput, calls=%fused_computation.99 | convolution fusion | flops 77070336 | bytes 376832 | tf_op jit(solution)/shard_map/tfc,btc->btf/dot_general | solution.py:91
  54.7 6.8 %fusion.4 = f32[64,4,192]{2,1,0:T(4,128)S(1)} fusion(s32[64,192]{1,0:T(8,128)S(1)} %get-tuple-element.48, f32[64,4,256]{2,1,0:T(4,128)S(1)} %gather_fusion), kind=kOutput, calls=%fused_computation.40 | convolution fusion | flops 154140672 | bytes 507904 | tf_op jit(solution)/shard_map/tfc,btc->btf/dot_general | solution.py:93
  61.5 6.9 %fusion.56 = f32[4,64,192]{2,0,1:T(4,128)S(1)} fusion(f32[64,4,192]{2,1,0:T(4,128)S(1)} %fusion.4, s32[64,192]{1,0:T(8,128)S(1)} %get-tuple-element.47, f32[4,1,128]{2,0,1:T(4,128)S(1)} %slice.454, f32[4,63,128]{2,0,1:T(4,128)S(1)} %slice.453, f32[4,64,128]{2,0,1:T(4,128)S(1)} %bitcast.444), kind=kOutput, calls=%fused_computation.94 | convolution fusion | flops 154320896 | bytes 704512 | tf_op jit(solution)/shard_map/tfc,btc->btf/dot_general | solution.py:92
  68.8 6.9 %fusion.50 = f32[5,64,256]{2,0,1:T(8,128)S(1)} fusion(s32[64,192]{1,0:T(8,128)S(1)} %get-tuple-element.47, f32[5,64,192]{2,1,0:T(8,128)S(1)} %maximum_multiply_fusion.1), kind=kOutput, calls=%fused_computation.88 | convolution fusion | flops 191889408 | bytes 622592 | tf_op jit(solution)/shard_map/tfc,btf->btc/dot_general | solution.py:101
  81.3 18.2 %all-reduce.5.cloned.1.call-done = f32[5,8192]{1,0:T(8,128)} async-done(((f32[5,8192]{1,0:T(8,128)}), f32[5,8192]{1,0:T(8,128)}) %all-reduce.5.cloned.1.call-update) | async-done | bytes 163856 | tf_op jit(solution)/shard_map/psum | solution.py:117
  123.0 6.4 %fusion.37 = f32[64,4,192]{2,1,0:T(4,128)S(1)} fusion(s32[64,192]{1,0:T(8,128)S(1)} %get-tuple-element.87, f32[1,64,128]{2,0,1:T(1,128)S(1)} %bitcast.423, f32[3,64,128]{2,0,1:T(4,128)S(1)} %bitcast.397), kind=kOutput, calls=%fused_computation.75 | convolution fusion | flops 77103104 | bytes 376832 | tf_op jit(solution)/shard_map/tfc,btc->btf/dot_general | solution.py:91
  145.3 6.8 %fusion.3 = f32[64,4,192]{2,1,0:T(4,128)S(1)} fusion(s32[64,192]{1,0:T(8,128)S(1)} %get-tuple-element.48, f32[64,4,256]{2,1,0:T(4,128)S(1)} %gather_fusion.1), kind=kOutput, calls=%fused_computation.39 | convolution fusion | flops 154140672 | bytes 507904 | tf_op jit(solution)/shard_map/tfc,btc->btf/dot_general | solution.py:93
  152.1 6.9 %fusion.57 = f32[64,4,192]{2,1,0:T(4,128)S(1)} fusion(f32[64,4,192]{2,1,0:T(4,128)S(1)} %fusion.3, s32[64,192]{1,0:T(8,128)S(1)} %get-tuple-element.47, f32[4,1,128]{2,0,1:T(4,128)S(1)} %fusion.167, f32[4,63,128]{2,0,1:T(4,128)S(1)} %fusion.154, f32[1,64,128]{2,0,1:T(1,128)S(1)} %bitcast.425, f32[3,64,128]{2,0,1:T(4,128)S(1)} %bitcast.399), kind=kOutput, calls=%fused_computation.95 | convolution fusion | flops 154386432 | bytes 704512 | tf_op jit(solution)/shard_map/tfc,btc->btf/dot_general | solution.py:92
  172.7 40.4 %all-reduce.2 = (f32[]{:T(128)}, f32[]{:T(128)}) all-reduce(f32[]{:T(128)} %get-tuple-element.16, f32[]{:T(128)} %get-tuple-element.15), channel_id=1, replica_groups=mesh['cells'=16,'faces'=2] {'cells'}, use_global_device_ids=true, to_apply=%region_1.2 | all-reduce | flops 2 | bytes 16 | tf_op jit(solution)/shard_map/psum | solution.py:147
  235.0 6.4 %fusion.35 = f32[64,4,192]{2,1,0:T(4,128)S(1)} fusion(s32[64,192]{1,0:T(8,128)S(1)} %get-tuple-element.87, f32[1,64,128]{2,0,1:T(1,128)S(1)} %bitcast.430, f32[3,64,128]{2,0,1:T(4,128)S(1)} %bitcast.401), kind=kOutput, calls=%fused_computation.73 | convolution fusion | flops 77103104 | bytes 376832 | tf_op jit(solution)/shard_map/tfc,btc->btf/dot_general | solution.py:91
  242.8 5.6 %collective-permute-start.15 = (f32[4,256]{1,0:T(4,128)S(1)}, f32[4,256]{1,0:T(4,128)S(1)}, u32[]{:S(2)}, u32[]{:S(2)}) collective-permute-start(f32[4,256]{1,0:T(4,128)S(1)} %get-tuple-element.63), channel_id=1, source_target_pairs={{2,0},{4,2},{6,4},{8,6},{10,8},{12,10},{14,12},{16,14},{18,16},{20... | collective-permute-start | bytes 12296 | tf_op jit(solution)/shard_map/ppermute | solution.py:13
  255.6 6.8 %fusion.2 = f32[64,4,192]{2,1,0:T(4,128)S(1)} fusion(s32[64,192]{1,0:T(8,128)S(1)} %get-tuple-element.48, f32[64,4,256]{2,1,0:T(4,128)S(1)} %gather_fusion.2), kind=kOutput, calls=%fused_computation.38 | convolution fusion | flops 154140672 | bytes 507904 | tf_op jit(solution)/shard_map/tfc,btc->btf/dot_general | solution.py:93
  262.4 6.9 %fusion.58 = f32[64,4,192]{2,1,0:T(4,128)S(1)} fusion(f32[64,4,192]{2,1,0:T(4,128)S(1)} %fusion.2, s32[64,192]{1,0:T(8,128)S(1)} %get-tuple-element.47, f32[4,1,128]{2,0,1:T(4,128)S(1)} %fusion.166, f32[4,63,128]{2,0,1:T(4,128)S(1)} %fusion.153, f32[1,64,128]{2,0,1:T(1,128)S(1)} %bitcast.432, f32[3,64,128]{2,0,1:T(4,128)S(1)} %bitcast.403), kind=kOutput, calls=%fused_computation.96 | convolution fusion | flops 154386432 | bytes 704512 | tf_op jit(solution)/shard_map/tfc,btc->btf/dot_general | solution.py:92
  283.1 40.8 %all-reduce.1 = (f32[]{:T(128)}, f32[]{:T(128)}, f32[]{:T(128)}, f32[]{:T(128)}) all-reduce(f32[]{:T(128)} %get-tuple-element.14, f32[]{:T(128)} %get-tuple-element.13, f32[]{:T(128)} %get-tuple-element.12, f32[]{:T(128)} %get-tuple-element.11), channel_id=1, replica_groups=mesh['cells'=16,'faces'=2] {'cells'}, use_global_device_ids=true, to_apply=%region_19.21 | all-reduce | flops 4 | bytes 32 | tf_op jit(solution)/shard_map/psum | solution.py:155
  350.1 6.4 %fusion.33 = f32[64,4,192]{2,1,0:T(4,128)S(1)} fusion(s32[64,192]{1,0:T(8,128)S(1)} %get-tuple-element.87, f32[1,64,128]{2,0,1:T(1,128)S(1)} %bitcast.415, f32[3,64,128]{2,0,1:T(4,128)S(1)} %bitcast.393), kind=kOutput, calls=%fused_computation.71 | convolution fusion | flops 77103104 | bytes 376832 | tf_op jit(solution)/shard_map/tfc,btc->btf/dot_general | solution.py:91
  358.0 5.6 %collective-permute-start.21 = (f32[4,256]{1,0:T(4,128)S(1)}, f32[4,256]{1,0:T(4,128)S(1)}, u32[]{:S(2)}, u32[]{:S(2)}) collective-permute-start(f32[4,256]{1,0:T(4,128)S(1)} %get-tuple-element.57), channel_id=1, source_target_pairs={{2,0},{4,2},{6,4},{8,6},{10,8},{12,10},{14,12},{16,14},{18,16},{20... | collective-permute-start | bytes 12296 | tf_op jit(solution)/shard_map/ppermute | solution.py:13
  370.7 6.8 %fusion.1 = f32[64,4,192]{2,1,0:T(4,128)S(1)} fusion(s32[64,192]{1,0:T(8,128)S(1)} %get-tuple-element.48, f32[64,4,256]{2,1,0:T(4,128)S(1)} %gather_fusion.3), kind=kOutput, calls=%fused_computation.37 | convolution fusion | flops 154140672 | bytes 507904 | tf_op jit(solution)/shard_map/tfc,btc->btf/dot_general | solution.py:93
  377.5 6.9 %fusion.59 = f32[64,4,192]{2,1,0:T(4,128)S(1)} fusion(f32[64,4,192]{2,1,0:T(4,128)S(1)} %fusion.1, s32[64,192]{1,0:T(8,128)S(1)} %get-tuple-element.47, f32[4,1,128]{2,0,1:T(4,128)S(1)} %fusion.165, f32[4,63,128]{2,0,1:T(4,128)S(1)} %fusion.152, f32[1,64,128]{2,0,1:T(1,128)S(1)} %bitcast.417, f32[3,64,128]{2,0,1:T(4,128)S(1)} %bitcast.395), kind=kOutput, calls=%fused_computation.97 | convolution fusion | flops 154386432 | bytes 704512 | tf_op jit(solution)/shard_map/tfc,btc->btf/dot_general | solution.py:92
  398.0 40.5 %psum.77 = f32[]{:T(128)} all-reduce(f32[]{:T(128)} %multiply_reduce_fusion.4), channel_id=1, replica_groups=mesh['cells'=16,'faces'=2] {'cells'}, use_global_device_ids=true, to_apply=%region_26.28 | all-reduce | flops 1 | bytes 8 | tf_op jit(solution)/shard_map/psum | solution.py:151
  459.8 6.4 %fusion.31 = f32[64,4,192]{2,1,0:T(4,128)S(1)} fusion(s32[64,192]{1,0:T(8,128)S(1)} %get-tuple-element.87, f32[1,64,128]{2,0,1:T(1,128)S(1)} %bitcast.437, f32[3,64,128]{2,0,1:T(4,128)S(1)} %bitcast.405), kind=kOutput, calls=%fused_computation.69 | convolution fusion | flops 77103104 | bytes 376832 | tf_op jit(solution)/shard_map/tfc,btc->btf/dot_general | solution.py:91
  467.7 5.6 %collective-permute-start.27 = (f32[4,256]{1,0:T(4,128)S(1)}, f32[4,256]{1,0:T(4,128)S(1)}, u32[]{:S(2)}, u32[]{:S(2)}) collective-permute-start(f32[4,256]{1,0:T(4,128)S(1)} %get-tuple-element.51), channel_id=1, source_target_pairs={{2,0},{4,2},{6,4},{8,6},{10,8},{12,10},{14,12},{16,14},{18,16},{20... | collective-permute-start | bytes 12296 | tf_op jit(solution)/shard_map/ppermute | solution.py:13
  480.4 6.8 %fusion = f32[64,4,192]{2,1,0:T(4,128)S(1)} fusion(s32[64,192]{1,0:T(8,128)S(1)} %get-tuple-element.48, f32[64,4,256]{2,1,0:T(4,128)S(1)} %gather_fusion.4), kind=kOutput, calls=%fused_computation.36 | convolution fusion | flops 154140672 | bytes 507904 | tf_op jit(solution)/shard_map/tfc,btc->btf/dot_general | solution.py:93
  487.2 6.9 %fusion.60 = f32[64,4,192]{2,1,0:T(4,128)S(1)} fusion(f32[64,4,192]{2,1,0:T(4,128)S(1)} %fusion, s32[64,192]{1,0:T(8,128)S(1)} %get-tuple-element.47, f32[4,1,128]{2,0,1:T(4,128)S(1)} %fusion.164, f32[4,63,128]{2,0,1:T(4,128)S(1)} %fusion.151, f32[1,64,128]{2,0,1:T(1,128)S(1)} %bitcast.439, f32[3,64,128]{2,0,1:T(4,128)S(1)} %bitcast.407), kind=kOutput, calls=%fused_computation.98 | convolution fusion | flops 154386432 | bytes 704512 | tf_op jit(solution)/shard_map/tfc,btc->btf/dot_general | solution.py:92
  507.8 40.5 %all-reduce = (f32[]{:T(128)}, f32[]{:T(128)}) all-reduce(f32[]{:T(128)} %get-tuple-element.10, f32[]{:T(128)} %get-tuple-element.9), channel_id=1, replica_groups=mesh['cells'=16,'faces'=2] {'cells'}, use_global_device_ids=true, to_apply=%region_31.33 | all-reduce | flops 2 | bytes 16 | tf_op jit(solution)/shard_map/psum | solution.py:155
  (377 shorter events, 228.6 us)
Async XLA Ops:
  7.2 92.2 %all-reduce.5.cloned.1.call-start = ((), (), s32[]{:S(2)}) async-start(), calls=%async_computation | async-start | bytes 524288 | tf_op jit(solution)/shard_map/psum | solution.py:117
  30.6 18.8 %collective-permute-start = (f32[4,256]{1,0:T(4,128)S(1)}, f32[4,256]{1,0:T(4,128)S(1)}, u32[]{:S(2)}, u32[]{:S(2)}) collective-permute-start(f32[4,256]{1,0:T(4,128)S(1)} %get-tuple-element.78), channel_id=1, source_target_pairs={{30,0},{0,2},{2,4},{4,6},{6,8},{8,10},{10,12},{12,14},{14,16},{16,... | collective-permute-start | bytes 12296 | tf_op jit(solution)/shard_map/ppermute | solution.py:13
  33.7 17.1 %collective-permute-start.1 = (f32[4,256]{1,0:T(4,128)S(1)}, f32[4,256]{1,0:T(4,128)S(1)}, u32[]{:S(2)}, u32[]{:S(2)}) collective-permute-start(f32[4,256]{1,0:T(4,128)S(1)} %get-tuple-element.77), channel_id=1, source_target_pairs={{28,0},{30,2},{0,4},{2,6},{4,8},{6,10},{8,12},{10,14},{12,16},{14,... | collective-permute-start | bytes 12296 | tf_op jit(solution)/shard_map/ppermute | solution.py:13
  35.2 15.6 %collective-permute-start.2 = (f32[4,256]{1,0:T(4,128)S(1)}, f32[4,256]{1,0:T(4,128)S(1)}, u32[]{:S(2)}, u32[]{:S(2)}) collective-permute-start(f32[4,256]{1,0:T(4,128)S(1)} %get-tuple-element.76), channel_id=1, source_target_pairs={{26,0},{28,2},{30,4},{0,6},{2,8},{4,10},{6,12},{8,14},{10,16},{12,... | collective-permute-start | bytes 12296 | tf_op jit(solution)/shard_map/ppermute | solution.py:13
  37.6 13.2 %collective-permute-start.3 = (f32[4,256]{1,0:T(4,128)S(1)}, f32[4,256]{1,0:T(4,128)S(1)}, u32[]{:S(2)}, u32[]{:S(2)}) collective-permute-start(f32[4,256]{1,0:T(4,128)S(1)} %get-tuple-element.75), channel_id=1, source_target_pairs={{2,0},{4,2},{6,4},{8,6},{10,8},{12,10},{14,12},{16,14},{18,16},{20... | collective-permute-start | bytes 12296 | tf_op jit(solution)/shard_map/ppermute | solution.py:13
  40.9 10.0 %collective-permute-start.4 = (f32[4,256]{1,0:T(4,128)S(1)}, f32[4,256]{1,0:T(4,128)S(1)}, u32[]{:S(2)}, u32[]{:S(2)}) collective-permute-start(f32[4,256]{1,0:T(4,128)S(1)} %get-tuple-element.74), channel_id=1, source_target_pairs={{4,0},{6,2},{8,4},{10,6},{12,8},{14,10},{16,12},{18,14},{20,16},{2... | collective-permute-start | bytes 12296 | tf_op jit(solution)/shard_map/ppermute | solution.py:13
  130.6 9.5 %collective-permute-start.6 = (f32[4,256]{1,0:T(4,128)S(1)}, f32[4,256]{1,0:T(4,128)S(1)}, u32[]{:S(2)}, u32[]{:S(2)}) collective-permute-start(f32[4,256]{1,0:T(4,128)S(1)} %get-tuple-element.72), channel_id=1, source_target_pairs={{30,0},{0,2},{2,4},{4,6},{6,8},{8,10},{10,12},{12,14},{14,16},{16,... | collective-permute-start | bytes 12296 | tf_op jit(solution)/shard_map/ppermute | solution.py:13
  132.4 8.8 %collective-permute-start.7 = (f32[4,256]{1,0:T(4,128)S(1)}, f32[4,256]{1,0:T(4,128)S(1)}, u32[]{:S(2)}, u32[]{:S(2)}) collective-permute-start(f32[4,256]{1,0:T(4,128)S(1)} %get-tuple-element.71), channel_id=1, source_target_pairs={{28,0},{30,2},{0,4},{2,6},{4,8},{6,10},{8,12},{10,14},{12,16},{14,... | collective-permute-start | bytes 12296 | tf_op jit(solution)/shard_map/ppermute | solution.py:13
  133.9 7.4 %collective-permute-start.8 = (f32[4,256]{1,0:T(4,128)S(1)}, f32[4,256]{1,0:T(4,128)S(1)}, u32[]{:S(2)}, u32[]{:S(2)}) collective-permute-start(f32[4,256]{1,0:T(4,128)S(1)} %get-tuple-element.70), channel_id=1, source_target_pairs={{26,0},{28,2},{30,4},{0,6},{2,8},{4,10},{6,12},{8,14},{10,16},{12,... | collective-permute-start | bytes 12296 | tf_op jit(solution)/shard_map/ppermute | solution.py:13
  136.3 5.0 collective-permute-start.9
  242.6 7.7 %collective-permute-start.12 = (f32[4,256]{1,0:T(4,128)S(1)}, f32[4,256]{1,0:T(4,128)S(1)}, u32[]{:S(2)}, u32[]{:S(2)}) collective-permute-start(f32[4,256]{1,0:T(4,128)S(1)} %get-tuple-element.66), channel_id=1, source_target_pairs={{30,0},{0,2},{2,4},{4,6},{6,8},{8,10},{10,12},{12,14},{14,16},{16,... | collective-permute-start | bytes 12296 | tf_op jit(solution)/shard_map/ppermute | solution.py:13
  242.7 10.6 %collective-permute-start.13 = (f32[4,256]{1,0:T(4,128)S(1)}, f32[4,256]{1,0:T(4,128)S(1)}, u32[]{:S(2)}, u32[]{:S(2)}) collective-permute-start(f32[4,256]{1,0:T(4,128)S(1)} %get-tuple-element.65), channel_id=1, source_target_pairs={{28,0},{30,2},{0,4},{2,6},{4,8},{6,10},{8,12},{10,14},{12,16},{14,... | collective-permute-start | bytes 12296 | tf_op jit(solution)/shard_map/ppermute | solution.py:13
  242.8 10.5 %collective-permute-start.14 = (f32[4,256]{1,0:T(4,128)S(1)}, f32[4,256]{1,0:T(4,128)S(1)}, u32[]{:S(2)}, u32[]{:S(2)}) collective-permute-start(f32[4,256]{1,0:T(4,128)S(1)} %get-tuple-element.64), channel_id=1, source_target_pairs={{26,0},{28,2},{30,4},{0,6},{2,8},{4,10},{6,12},{8,14},{10,16},{12,... | collective-permute-start | bytes 12296 | tf_op jit(solution)/shard_map/ppermute | solution.py:13
  242.8 10.5 %collective-permute-start.15 = (f32[4,256]{1,0:T(4,128)S(1)}, f32[4,256]{1,0:T(4,128)S(1)}, u32[]{:S(2)}, u32[]{:S(2)}) collective-permute-start(f32[4,256]{1,0:T(4,128)S(1)} %get-tuple-element.63), channel_id=1, source_target_pairs={{2,0},{4,2},{6,4},{8,6},{10,8},{12,10},{14,12},{16,14},{18,16},{20... | collective-permute-start | bytes 12296 | tf_op jit(solution)/shard_map/ppermute | solution.py:13
  357.8 7.7 %collective-permute-start.18 = (f32[4,256]{1,0:T(4,128)S(1)}, f32[4,256]{1,0:T(4,128)S(1)}, u32[]{:S(2)}, u32[]{:S(2)}) collective-permute-start(f32[4,256]{1,0:T(4,128)S(1)} %get-tuple-element.60), channel_id=1, source_target_pairs={{30,0},{0,2},{2,4},{4,6},{6,8},{8,10},{10,12},{12,14},{14,16},{16,... | collective-permute-start | bytes 12296 | tf_op jit(solution)/shard_map/ppermute | solution.py:13
  357.9 10.6 %collective-permute-start.19 = (f32[4,256]{1,0:T(4,128)S(1)}, f32[4,256]{1,0:T(4,128)S(1)}, u32[]{:S(2)}, u32[]{:S(2)}) collective-permute-start(f32[4,256]{1,0:T(4,128)S(1)} %get-tuple-element.59), channel_id=1, source_target_pairs={{28,0},{30,2},{0,4},{2,6},{4,8},{6,10},{8,12},{10,14},{12,16},{14,... | collective-permute-start | bytes 12296 | tf_op jit(solution)/shard_map/ppermute | solution.py:13
  357.9 10.5 %collective-permute-start.20 = (f32[4,256]{1,0:T(4,128)S(1)}, f32[4,256]{1,0:T(4,128)S(1)}, u32[]{:S(2)}, u32[]{:S(2)}) collective-permute-start(f32[4,256]{1,0:T(4,128)S(1)} %get-tuple-element.58), channel_id=1, source_target_pairs={{26,0},{28,2},{30,4},{0,6},{2,8},{4,10},{6,12},{8,14},{10,16},{12,... | collective-permute-start | bytes 12296 | tf_op jit(solution)/shard_map/ppermute | solution.py:13
  358.0 10.5 %collective-permute-start.21 = (f32[4,256]{1,0:T(4,128)S(1)}, f32[4,256]{1,0:T(4,128)S(1)}, u32[]{:S(2)}, u32[]{:S(2)}) collective-permute-start(f32[4,256]{1,0:T(4,128)S(1)} %get-tuple-element.57), channel_id=1, source_target_pairs={{2,0},{4,2},{6,4},{8,6},{10,8},{12,10},{14,12},{16,14},{18,16},{20... | collective-permute-start | bytes 12296 | tf_op jit(solution)/shard_map/ppermute | solution.py:13
  363.6 4.9 collective-permute-start.22
  467.5 7.7 %collective-permute-start.24 = (f32[4,256]{1,0:T(4,128)S(1)}, f32[4,256]{1,0:T(4,128)S(1)}, u32[]{:S(2)}, u32[]{:S(2)}) collective-permute-start(f32[4,256]{1,0:T(4,128)S(1)} %get-tuple-element.54), channel_id=1, source_target_pairs={{30,0},{0,2},{2,4},{4,6},{6,8},{8,10},{10,12},{12,14},{14,16},{16,... | collective-permute-start | bytes 12296 | tf_op jit(solution)/shard_map/ppermute | solution.py:13
  467.6 10.6 %collective-permute-start.25 = (f32[4,256]{1,0:T(4,128)S(1)}, f32[4,256]{1,0:T(4,128)S(1)}, u32[]{:S(2)}, u32[]{:S(2)}) collective-permute-start(f32[4,256]{1,0:T(4,128)S(1)} %get-tuple-element.53), channel_id=1, source_target_pairs={{28,0},{30,2},{0,4},{2,6},{4,8},{6,10},{8,12},{10,14},{12,16},{14,... | collective-permute-start | bytes 12296 | tf_op jit(solution)/shard_map/ppermute | solution.py:13
  467.6 10.5 %collective-permute-start.26 = (f32[4,256]{1,0:T(4,128)S(1)}, f32[4,256]{1,0:T(4,128)S(1)}, u32[]{:S(2)}, u32[]{:S(2)}) collective-permute-start(f32[4,256]{1,0:T(4,128)S(1)} %get-tuple-element.52), channel_id=1, source_target_pairs={{26,0},{28,2},{30,4},{0,6},{2,8},{4,10},{6,12},{8,14},{10,16},{12,... | collective-permute-start | bytes 12296 | tf_op jit(solution)/shard_map/ppermute | solution.py:13
  467.7 10.5 %collective-permute-start.27 = (f32[4,256]{1,0:T(4,128)S(1)}, f32[4,256]{1,0:T(4,128)S(1)}, u32[]{:S(2)}, u32[]{:S(2)}) collective-permute-start(f32[4,256]{1,0:T(4,128)S(1)} %get-tuple-element.51), channel_id=1, source_target_pairs={{2,0},{4,2},{6,4},{8,6},{10,8},{12,10},{14,12},{16,14},{18,16},{20... | collective-permute-start | bytes 12296 | tf_op jit(solution)/shard_map/ppermute | solution.py:13
  473.3 4.9 collective-permute-start.28
  (16 other events, 350.9 us)
Sparse Core Ops, SparseCore 0:
  81.3 18.0 all-reduce.4
